TPU v7x, 32 devices: a whole 2x2x4 slice. The times are simulated.
32 devices in a mesh: row: 4 (over z), col: 8 (over y, x, core).
Axes of the slice: x: 2, y: 2, z: 4, core: 2. Of those that a mesh axis runs over, the one named last changes fastest.
Arguments:
- minus_gradient: float32 [6, 16384], P(None, ('row', 'col')), may hold values from -10 to 10
- diag_blocks: float32 [36, 16384], P(None, ('row', 'col')), may hold values from -1000 to 1000, as said below
- hess_blocks: float32 [4, 8, 36, 4096], P('row', 'col'), may hold values from -40 to 40, as said below
- block_rows: int32 [4, 8, 4096], P('row', 'col'), may hold values from 0 to 2047
- block_cols: int32 [4, 8, 4096], P('row', 'col'), may hold values from 0 to 4095
- block_counts: int32 [4, 8], P('row', 'col'), may hold values from 0 to 4096, as said below
Outputs:
- pose_update: float32 [6, 16384], P(None, ('row', 'col'))
- residual: float32 [6, 16384], P(None, ('row', 'col'))
Inputs may be any that keep to these rules, and one draw needn't show every extreme that they name: `hess_blocks`: the live blocks of all tiles together with diag_blocks form a symmetric positive definite matrix; no live block lies on the diagonal; the slots after the live ones hold arbitrary entries. `diag_blocks`: each 6x6 block is symmetric positive definite. The live slots of a tile are its first block_counts slots.
All inputs are finite; a program needn't handle non-finite values.
Results may differ from a plain program's by a relative error of at most 0.0003.
Values sent between devices are 32-bit elements; how exact they have to be, the bound alone decides.
No kernel may reach another device: no remote copies, remote signals or barrier semaphores. Data moves between devices by JAX's collectives and lax.ppermute only.
A program may use at most 64 MiB of HBM per device.

v0:
```python
import math
import jax
import jax.numpy as jnp
from jax import lax
from jax.sharding import PartitionSpec as P

ITERS = 3


def factor_blocks(blocks):
    lower_part = {}
    reciprocals = []
    for j in range(6):
        pivot_value = blocks[7 * j]
        for k in range(j):
            pivot_value = pivot_value - lower_part[j, k] * lower_part[j, k]
        reciprocal = 1.0 / jnp.sqrt(pivot_value)
        reciprocals.append(reciprocal)
        for i in range(j + 1, 6):
            entry_value = blocks[6 * i + j]
            for k in range(j):
                entry_value = entry_value - lower_part[i, k] * lower_part[j, k]
            lower_part[i, j] = entry_value * reciprocal
    return (lower_part, reciprocals)


def apply_inverse(lower_part, reciprocals, vector):
    forward = []
    for i in range(6):
        running = vector[i]
        for k in range(i):
            running = running - lower_part[i, k] * forward[k]
        forward.append(running * reciprocals[i])
    backward = [None] * 6
    for i in range(5, -1, -1):
        running = forward[i]
        for k in range(i + 1, 6):
            running = running - lower_part[k, i] * backward[k]
        backward[i] = running * reciprocals[i]
    return jnp.stack(backward)


def diagonal_term(diag_blocks, vector):
    return jnp.sum(diag_blocks.reshape(6, 6, -1) * vector[None], axis=1)


def pick_columns(source, offsets):
    width = source.shape[1]
    low_width = math.gcd(128, width)
    high_width = width // low_width
    table = source.reshape(6 * high_width, low_width)
    slot_count = offsets.shape[0]
    block_size = math.gcd(512, slot_count)
    turns = slot_count // block_size

    def pick_one_block(carry, offset):
        low_part = offset % low_width
        high_part = offset // low_width
        low_onehot = (
            lax.broadcasted_iota(jnp.int32, (low_width, block_size), 0) == low_part[None, :]
        ).astype(jnp.float32)
        spread = jnp.dot(
            table, low_onehot, precision=lax.Precision.HIGHEST, preferred_element_type=jnp.float32
        )
        high_onehot = (
            lax.broadcasted_iota(jnp.int32, (high_width, block_size), 0) == high_part[None, :]
        ).astype(jnp.float32)
        chosen = jnp.sum(spread.reshape(6, high_width, block_size) * high_onehot[None], axis=1)
        return (carry, chosen)

    unused, blocks_out = lax.scan(pick_one_block, None, offsets.reshape(turns, block_size))
    return jnp.transpose(blocks_out, (1, 0, 2)).reshape(6, slot_count)


def add_rows(terms, rows, span_size):
    low_width = math.gcd(128, span_size)
    high_width = span_size // low_width
    slot_count = rows.shape[0]
    block_size = math.gcd(512, slot_count)
    turns = slot_count // block_size
    term_blocks = jnp.transpose(terms.reshape(6, turns, block_size), (1, 0, 2))
    row_blocks = rows.reshape(turns, block_size)

    def add_one_block(carry, inputs):
        term_block, row_block = inputs
        high_onehot = (
            lax.broadcasted_iota(jnp.int32, (high_width, block_size), 0)
            == (row_block // low_width)[None, :]
        ).astype(jnp.float32)
        spread = (term_block[:, None, :] * high_onehot[None]).reshape(6 * high_width, block_size)
        low_onehot = (
            (row_block % low_width)[:, None]
            == lax.broadcasted_iota(jnp.int32, (block_size, low_width), 1)
        ).astype(jnp.float32)
        carry = carry + jnp.dot(
            spread, low_onehot, precision=lax.Precision.HIGHEST, preferred_element_type=jnp.float32
        )
        return (carry, None)

    start_total = jnp.zeros((6 * high_width, low_width), jnp.float32)
    total, unused = lax.scan(add_one_block, start_total, (term_blocks, row_blocks))
    return total.reshape(6, span_size)


def merged_sums(residual, precond, hess_image):
    return lax.psum((jnp.sum(residual * precond), jnp.sum(hess_image * precond)), ("row", "col"))


def on_device(minus_gradient, diag_blocks, hess_blocks, block_rows, block_cols, block_counts):
    pose_dev = minus_gradient.shape[1]
    blocks = hess_blocks.reshape(6, 6, -1)
    local_rows = block_rows.reshape(-1)
    local_cols = block_cols.reshape(-1)
    slot_count = local_rows.shape[0]
    live_mask = jnp.arange(slot_count, dtype=jnp.int32) < block_counts.reshape(())
    span_size = pose_dev * lax.axis_size("row")
    lower_part, reciprocals = factor_blocks(diag_blocks)

    def tile_terms(picked):
        return jnp.sum(blocks * picked[None], axis=1)

    def hessian(vector):
        gathered = lax.all_gather(vector, "col", axis=1, tiled=True)
        picked = pick_columns(gathered, local_cols)
        live_terms = jnp.where(live_mask[None, :], tile_terms(picked), 0.0)
        partial_value = add_rows(live_terms, local_rows, span_size)
        own_term = diagonal_term(diag_blocks, vector)
        summed = lax.psum(partial_value, "row")
        reduced = lax.dynamic_slice_in_dim(summed, lax.axis_index("row") * pose_dev, pose_dev, 1)
        return reduced + own_term

    solution = jnp.zeros_like(minus_gradient)
    residual = minus_gradient
    precond = apply_inverse(lower_part, reciprocals, residual)
    hess_image = hessian(precond)
    rho_now, curv_value = merged_sums(residual, precond, hess_image)
    step_size = rho_now / curv_value
    direction = precond
    along_image = hess_image
    for k in range(ITERS):
        solution = solution + step_size * direction
        residual = residual - step_size * along_image
        if k + 1 < ITERS:
            precond = apply_inverse(lower_part, reciprocals, residual)
            hess_image = hessian(precond)
            rho_next, curv_value = merged_sums(residual, precond, hess_image)
            ratio_next = rho_next / rho_now
            step_size = rho_next / (curv_value - ratio_next * rho_next / step_size)
            direction = precond + ratio_next * direction
            along_image = hess_image + ratio_next * along_image
            rho_now = rho_next
    return (solution, residual)


def solution(mesh):
    placed = (
        P(None, ("row", "col")),
        P(None, ("row", "col")),
        P("row", "col", None, None),
        P("row", "col", None),
        P("row", "col", None),
        P("row", "col"),
    )
    return jax.shard_map(
        on_device,
        mesh=mesh,
        in_specs=placed,
        out_specs=(P(None, ("row", "col")), P(None, ("row", "col"))),
        check_vma=False,
    )
```

profile of v0, /device:TPU:14, one launch (start us, length us, event | category | flops | bytes accessed | tf_op | source)
XLA Modules:
  0.0 246.8 jit_solution(5160269623161957242)
XLA Ops:
  0.6 1.1 subtract_multiply_fusion.21
  1.7 0.7 copy-done.2
  2.6 8.2 %all_gather.9 = f32[6,4096]{1,0:T(8,128)S(1)} all-gather(f32[6,512]{1,0:T(8,128)S(1)} %stack.6), channel_id=1, replica_groups=mesh['row'=4,'col'=8] {'col'}, dimensions={1}, use_global_device_ids=true | all-gather | bytes 110592 | tf_op jit(solution)/shard_map/all_gather | solution.py:123
  11.5 0.7 reduce.7
  12.3 3.9 %while.75 = (s32[]{:T(128)}, f32[8,6,512]{2,1,0:T(8,128)S(1)}, s32[8,512]{1,0:T(8,128)S(1)}, f32[192,128]{1,0:T(8,128)S(1)}, s32[]{:T(128)}) while((s32[]{:T(128)}, f32[8,6,512]{2,1,0:T(8,128)S(1)}, s32[8,512]{1,0:T(8,128)S(1)}, f32[192,128]{1,0:T(8,128)S(1)}, s32[]{:T(128)}) %tuple.218), condition=%wide.region_4.5_spmd, body=%wide.region_2.4_spmd.sunk | while | flops 151297024 | bytes 1075269 | solution.py:71
  16.2 1.4 reduce
  18.7 0.7 copy-done.4
  19.4 0.7 reduce.8
  20.1 3.9 %while.78 = (s32[]{:T(128)}, f32[96,128]{1,0:T(8,128)S(1)}, f32[8,6,512]{2,1,0:T(8,128)S(1)}, s32[8,512]{1,0:T(8,128)S(1)}, s32[]{:T(128)}, /*index=5*/s32[]{:T(128)}) while((s32[]{:T(128)}, f32[96,128]{1,0:T(8,128)S(1)}, f32[8,6,512]{2,1,0:T(8,128)S(1)}, s32[8,512]{1,0:T(8,128)S(1)}, s32[]{:T(128)}, /*index=5*/s32[]{:T(128)}) %tuple.221), condition=%wide.region_7.8_spmd.clone, body=%wide.region_6.7_spmd.clone.sunk | while | flops 75666432 | bytes 608343 | solution.py:101
  24.0 16.2 %psum.64 = f32[6,2048]{1,0:T(8,128)S(1)} all-reduce(f32[6,2048]{1,0:T(8,128)S(1)} %reshape.316), channel_id=1, replica_groups=mesh['row'=4,'col'=8] {'row'}, use_global_device_ids=true, to_apply=%region_8.9 | all-reduce | flops 12288 | bytes 98304 | tf_op jit(solution)/shard_map/psum | solution.py:128
  40.9 44.0 %all-reduce.2 = (f32[]{:T(128)}, f32[]{:T(128)}) all-reduce(f32[]{:T(128)} %get-tuple-element.394, f32[]{:T(128)} %get-tuple-element.393), channel_id=1, replica_groups=mesh['row'=4,'col'=8] {'row','col'}, use_global_device_ids=true, to_apply=%region_1.2 | all-reduce | flops 2 | bytes 16 | tf_op jit(solution)/shard_map/psum | solution.py:106
  86.4 8.2 %all_gather.10 = f32[6,4096]{1,0:T(8,128)S(1)} all-gather(f32[6,512]{1,0:T(8,128)S(1)} %stack.7), channel_id=1, replica_groups=mesh['row'=4,'col'=8] {'col'}, dimensions={1}, use_global_device_ids=true | all-gather | bytes 110592 | tf_op jit(solution)/shard_map/all_gather | solution.py:123
  94.6 3.9 %while.76 = (s32[]{:T(128)}, f32[8,6,512]{2,1,0:T(8,128)S(1)}, s32[8,512]{1,0:T(8,128)S(1)}, f32[192,128]{1,0:T(8,128)S(1)}, s32[]{:T(128)}) while((s32[]{:T(128)}, f32[8,6,512]{2,1,0:T(8,128)S(1)}, s32[8,512]{1,0:T(8,128)S(1)}, f32[192,128]{1,0:T(8,128)S(1)}, s32[]{:T(128)}) %tuple.236), condition=%wide.region_16.17_spmd, body=%wide.region_14.16_spmd.sunk | while | flops 151297024 | bytes 1075269 | solution.py:71
  98.9 3.9 %while.79 = (s32[]{:T(128)}, f32[96,128]{1,0:T(8,128)S(1)}, f32[8,6,512]{2,1,0:T(8,128)S(1)}, s32[8,512]{1,0:T(8,128)S(1)}, s32[]{:T(128)}, /*index=5*/s32[]{:T(128)}) while((s32[]{:T(128)}, f32[96,128]{1,0:T(8,128)S(1)}, f32[8,6,512]{2,1,0:T(8,128)S(1)}, s32[8,512]{1,0:T(8,128)S(1)}, s32[]{:T(128)}, ...), condition=%wide.region_19.20_spmd.clone, body=%wide.region_18.19_spmd.clone.sunk | while | flops 75666432 | bytes 608343 | solution.py:101
  102.8 14.3 %psum.67 = f32[6,2048]{1,0:T(8,128)S(1)} all-reduce(f32[6,2048]{1,0:T(8,128)S(1)} %reshape.319), channel_id=1, replica_groups=mesh['row'=4,'col'=8] {'row'}, use_global_device_ids=true, to_apply=%region_20.21 | all-reduce | flops 12288 | bytes 98304 | tf_op jit(solution)/shard_map/psum | solution.py:128
  117.1 0.7 multiply_reduce_fusion.11
  117.8 44.2 %all-reduce.1 = (f32[]{:T(128)}, f32[]{:T(128)}) all-reduce(f32[]{:T(128)} %get-tuple-element.392, f32[]{:T(128)} %get-tuple-element.391), channel_id=1, replica_groups=mesh['row'=4,'col'=8] {'row','col'}, use_global_device_ids=true, to_apply=%region_13.14 | all-reduce | flops 2 | bytes 16 | tf_op jit(solution)/shard_map/psum | solution.py:106
  166.7 8.1 %all_gather.11 = f32[6,4096]{1,0:T(8,128)S(1)} all-gather(f32[6,512]{1,0:T(8,128)S(1)} %stack.8), channel_id=1, replica_groups=mesh['row'=4,'col'=8] {'col'}, dimensions={1}, use_global_device_ids=true | all-gather | bytes 110592 | tf_op jit(solution)/shard_map/all_gather | solution.py:123
  174.9 3.9 %while.77 = (s32[]{:T(128)}, f32[8,6,512]{2,1,0:T(8,128)S(1)}, s32[8,512]{1,0:T(8,128)S(1)}, f32[192,128]{1,0:T(8,128)S(1)}, s32[]{:T(128)}) while((s32[]{:T(128)}, f32[8,6,512]{2,1,0:T(8,128)S(1)}, s32[8,512]{1,0:T(8,128)S(1)}, f32[192,128]{1,0:T(8,128)S(1)}, s32[]{:T(128)}) %tuple.237), condition=%wide.region_28.29_spmd, body=%wide.region_26.28_spmd.sunk | while | flops 151297024 | bytes 1075269 | solution.py:71
  179.1 3.9 %while.80 = (s32[]{:T(128)}, f32[96,128]{1,0:T(8,128)S(1)}, f32[8,6,512]{2,1,0:T(8,128)S(1)}, s32[8,512]{1,0:T(8,128)S(1)}, s32[]{:T(128)}, /*index=5*/s32[]{:T(128)}) while((s32[]{:T(128)}, f32[96,128]{1,0:T(8,128)S(1)}, f32[8,6,512]{2,1,0:T(8,128)S(1)}, s32[8,512]{1,0:T(8,128)S(1)}, s32[]{:T(128)}, ...), condition=%wide.region_31.32_spmd.clone, body=%wide.region_30.31_spmd.clone.sunk | while | flops 75666432 | bytes 608343 | solution.py:101
  183.0 14.4 %psum.70 = f32[6,2048]{1,0:T(8,128)S(1)} all-reduce(f32[6,2048]{1,0:T(8,128)S(1)} %reshape.321), channel_id=1, replica_groups=mesh['row'=4,'col'=8] {'row'}, use_global_device_ids=true, to_apply=%region_32.33 | all-reduce | flops 12288 | bytes 98304 | tf_op jit(solution)/shard_map/psum | solution.py:128
  197.5 0.6 multiply_reduce_fusion.9
  198.1 44.1 %all-reduce = (f32[]{:T(128)}, f32[]{:T(128)}) all-reduce(f32[]{:T(128)} %get-tuple-element.390, f32[]{:T(128)} %get-tuple-element.389), channel_id=1, replica_groups=mesh['row'=4,'col'=8] {'row','col'}, use_global_device_ids=true, to_apply=%region_25.26 | all-reduce | flops 2 | bytes 16 | tf_op jit(solution)/shard_map/psum | solution.py:106
  246.2 0.6 multiply_subtract_fusion
  (334 shorter events, 23.5 us)
Async XLA Ops:
  0.6 1.1 copy-start.1
  1.7 0.7 copy-start.2
  10.8 0.7 copy-start.3
  12.2 4.0 %copy-start = (f32[1,1,36,4096]{3,1,2,0:T(1,128)S(1)}, f32[1,1,36,4096]{3,1,2,0:T(1,128)}, u32[]{:S(2)}) copy-start(f32[1,1,36,4096]{3,1,2,0:T(1,128)} %param.20) | copy-start | bytes 1769476
  18.6 0.7 copy-start.4
where the time goes:
time: 248 us; the launch traced here: 247 us
  blocking collectives  202 us (81%)
  matrix products  16.6 us (7%)
  between operations  11.5 us (5%)
  other arithmetic  11.1 us (4%)
  loops' own time  2.93 us (1%)
  local copies, waits for them, and re-layouts  2.92 us (1%)
    psum x3, blocking collectives, merged_sums(): lax.psum((jnp.sum(residual * precond), jnp.sum(hess_image * precond)), ('...  132 us
    psum x3, blocking collectives, hessian(): summed = lax.psum(partial_value, 'row')  44.9 us
    all_gather x3, blocking collectives, hessian(): gathered = lax.all_gather(vector, 'col', axis=1, tiled=True)  24.5 us
    dot_general x24, matrix products, add_one_block(): jnp.dot(spread, low_onehot, precision=lax.Precision.HIGHEST, preferred_el...  8.61 us
    dot_general x24, matrix products, pick_one_block(): jnp.dot(table, low_onehot, precision=lax.Precision.HIGHEST, preferred_ele...  7.99 us

commit v1 on v0

--- a/solution.py
+++ b/solution.py
@@ -125,7 +125,7 @@
         live_terms = jnp.where(live_mask[None, :], tile_terms(picked), 0.0)
         partial_value = add_rows(live_terms, local_rows, span_size)
         own_term = diagonal_term(diag_blocks, vector)
-        summed = lax.psum(partial_value, "row")
+        summed = jnp.sum(lax.all_gather(partial_value, "row"), axis=0)
         reduced = lax.dynamic_slice_in_dim(summed, lax.axis_index("row") * pose_dev, pose_dev, 1)
         return reduced + own_term
 

time: 248 us -> 236 us (0.952)
  blocking collectives: 202 us -> 189 us
    psum x3 -> x0, blocking collectives: 44.9 us -> none  [hessian(): summed = lax.psum(partial_value, 'row')]
    all_gather x0 -> x3, blocking collectives: none -> 39 us  [hessian(): summed = jnp.sum(lax.all_gather(partial_value, 'row'), axis=0)]
    psum x3, blocking collectives: 132 us -> 125 us  [merged_sums(): lax.psum((jnp.sum(residual * precond), jnp.sum(hess_image * precond)), ('...]
where the time goes in v1:
time: 236 us; the launch traced here: 234 us
  blocking collectives  189 us (80%)
  matrix products  16.6 us (7%)
  between operations  11.5 us (5%)
  other arithmetic  11.2 us (5%)
  loops' own time  2.93 us (1%)
  local copies, waits for them, and re-layouts  2.92 us (1%)
    psum x3, blocking collectives, merged_sums(): lax.psum((jnp.sum(residual * precond), jnp.sum(hess_image * precond)), ('...  125 us
    all_gather x3, blocking collectives, hessian(): summed = jnp.sum(lax.all_gather(partial_value, 'row'), axis=0)  39 us
    all_gather x3, blocking collectives, hessian(): gathered = lax.all_gather(vector, 'col', axis=1, tiled=True)  24.6 us
    dot_general x24, matrix products, add_one_block(): jnp.dot(spread, low_onehot, precision=lax.Precision.HIGHEST, preferred_el...  8.61 us
    dot_general x24, matrix products, pick_one_block(): jnp.dot(table, low_onehot, precision=lax.Precision.HIGHEST, preferred_ele...  7.98 us

profile of v1, /device:TPU:14, one launch (start us, length us, event | category | flops | bytes accessed | tf_op | source)
XLA Modules:
  0.0 234.0 jit_solution(4235402984477237381)
XLA Ops:
  0.6 1.1 subtract_multiply_fusion.21
  1.7 0.7 copy-done.2
  2.6 8.2 %all_gather.18 = f32[6,4096]{1,0:T(8,128)S(1)} all-gather(f32[6,512]{1,0:T(8,128)S(1)} %stack.6), channel_id=1, replica_groups=mesh['row'=4,'col'=8] {'col'}, dimensions={1}, use_global_device_ids=true | all-gather | bytes 110592 | tf_op jit(solution)/shard_map/all_gather | solution.py:123
  11.5 0.7 reduce.7
  12.3 3.9 %while.75 = (s32[]{:T(128)}, f32[8,6,512]{2,1,0:T(8,128)S(1)}, s32[8,512]{1,0:T(8,128)S(1)}, f32[192,128]{1,0:T(8,128)S(1)}, s32[]{:T(128)}) while((s32[]{:T(128)}, f32[8,6,512]{2,1,0:T(8,128)S(1)}, s32[8,512]{1,0:T(8,128)S(1)}, f32[192,128]{1,0:T(8,128)S(1)}, s32[]{:T(128)}) %tuple.218), condition=%wide.region_4.5_spmd, body=%wide.region_2.4_spmd.sunk | while | flops 151297024 | bytes 1075269 | solution.py:71
  16.2 1.4 reduce
  18.7 0.7 copy-done.4
  19.4 0.7 reduce.8
  20.1 3.9 %while.78 = (s32[]{:T(128)}, f32[96,128]{1,0:T(8,128)S(1)}, f32[8,6,512]{2,1,0:T(8,128)S(1)}, s32[8,512]{1,0:T(8,128)S(1)}, s32[]{:T(128)}, /*index=5*/s32[]{:T(128)}) while((s32[]{:T(128)}, f32[96,128]{1,0:T(8,128)S(1)}, f32[8,6,512]{2,1,0:T(8,128)S(1)}, s32[8,512]{1,0:T(8,128)S(1)}, s32[]{:T(128)}, /*index=5*/s32[]{:T(128)}) %tuple.221), condition=%wide.region_7.8_spmd.clone, body=%wide.region_6.7_spmd.clone.sunk | while | flops 75666432 | bytes 608343 | solution.py:101
  24.0 14.6 %all_gather.19 = f32[4,6,2048]{2,1,0:T(8,128)S(1)} all-gather(f32[1,6,2048]{2,1,0:T(8,128)S(1)} %all_gather_reshape.9), channel_id=1, replica_groups=mesh['row'=4,'col'=8] {'row'}, dimensions={0}, use_global_device_ids=true | all-gather | bytes 245760 | tf_op jit(solution)/shard_map/all_gather | solution.py:128
  39.3 41.5 %all-reduce.2 = (f32[]{:T(128)}, f32[]{:T(128)}) all-reduce(f32[]{:T(128)} %get-tuple-element.394, f32[]{:T(128)} %get-tuple-element.393), channel_id=1, replica_groups=mesh['row'=4,'col'=8] {'row','col'}, use_global_device_ids=true, to_apply=%region_1.2 | all-reduce | flops 2 | bytes 16 | tf_op jit(solution)/shard_map/psum | solution.py:106
  82.3 8.2 %all_gather.20 = f32[6,4096]{1,0:T(8,128)S(1)} all-gather(f32[6,512]{1,0:T(8,128)S(1)} %stack.7), channel_id=1, replica_groups=mesh['row'=4,'col'=8] {'col'}, dimensions={1}, use_global_device_ids=true | all-gather | bytes 110592 | tf_op jit(solution)/shard_map/all_gather | solution.py:123
  90.6 3.9 %while.76 = (s32[]{:T(128)}, f32[8,6,512]{2,1,0:T(8,128)S(1)}, s32[8,512]{1,0:T(8,128)S(1)}, f32[192,128]{1,0:T(8,128)S(1)}, s32[]{:T(128)}) while((s32[]{:T(128)}, f32[8,6,512]{2,1,0:T(8,128)S(1)}, s32[8,512]{1,0:T(8,128)S(1)}, f32[192,128]{1,0:T(8,128)S(1)}, s32[]{:T(128)}) %tuple.236), condition=%wide.region_16.17_spmd, body=%wide.region_14.16_spmd.sunk | while | flops 151297024 | bytes 1075269 | solution.py:71
  94.8 3.9 %while.79 = (s32[]{:T(128)}, f32[96,128]{1,0:T(8,128)S(1)}, f32[8,6,512]{2,1,0:T(8,128)S(1)}, s32[8,512]{1,0:T(8,128)S(1)}, s32[]{:T(128)}, /*index=5*/s32[]{:T(128)}) while((s32[]{:T(128)}, f32[96,128]{1,0:T(8,128)S(1)}, f32[8,6,512]{2,1,0:T(8,128)S(1)}, s32[8,512]{1,0:T(8,128)S(1)}, s32[]{:T(128)}, ...), condition=%wide.region_19.20_spmd.clone, body=%wide.region_18.19_spmd.clone.sunk | while | flops 75666432 | bytes 608343 | solution.py:101
  98.7 12.2 %all_gather.21 = f32[4,6,2048]{2,1,0:T(8,128)S(1)} all-gather(f32[1,6,2048]{2,1,0:T(8,128)S(1)} %all_gather_reshape.10), channel_id=1, replica_groups=mesh['row'=4,'col'=8] {'row'}, dimensions={0}, use_global_device_ids=true | all-gather | bytes 245760 | tf_op jit(solution)/shard_map/all_gather | solution.py:128
  111.0 0.7 multiply_reduce_fusion.11
  111.7 42.2 %all-reduce.1 = (f32[]{:T(128)}, f32[]{:T(128)}) all-reduce(f32[]{:T(128)} %get-tuple-element.392, f32[]{:T(128)} %get-tuple-element.391), channel_id=1, replica_groups=mesh['row'=4,'col'=8] {'row','col'}, use_global_device_ids=true, to_apply=%region_13.14 | all-reduce | flops 2 | bytes 16 | tf_op jit(solution)/shard_map/psum | solution.py:106
  158.6 8.2 %all_gather.22 = f32[6,4096]{1,0:T(8,128)S(1)} all-gather(f32[6,512]{1,0:T(8,128)S(1)} %stack.8), channel_id=1, replica_groups=mesh['row'=4,'col'=8] {'col'}, dimensions={1}, use_global_device_ids=true | all-gather | bytes 110592 | tf_op jit(solution)/shard_map/all_gather | solution.py:123
  166.8 3.9 %while.77 = (s32[]{:T(128)}, f32[8,6,512]{2,1,0:T(8,128)S(1)}, s32[8,512]{1,0:T(8,128)S(1)}, f32[192,128]{1,0:T(8,128)S(1)}, s32[]{:T(128)}) while((s32[]{:T(128)}, f32[8,6,512]{2,1,0:T(8,128)S(1)}, s32[8,512]{1,0:T(8,128)S(1)}, f32[192,128]{1,0:T(8,128)S(1)}, s32[]{:T(128)}) %tuple.237), condition=%wide.region_28.29_spmd, body=%wide.region_26.28_spmd.sunk | while | flops 151297024 | bytes 1075269 | solution.py:71
  171.1 3.9 %while.80 = (s32[]{:T(128)}, f32[96,128]{1,0:T(8,128)S(1)}, f32[8,6,512]{2,1,0:T(8,128)S(1)}, s32[8,512]{1,0:T(8,128)S(1)}, s32[]{:T(128)}, /*index=5*/s32[]{:T(128)}) while((s32[]{:T(128)}, f32[96,128]{1,0:T(8,128)S(1)}, f32[8,6,512]{2,1,0:T(8,128)S(1)}, s32[8,512]{1,0:T(8,128)S(1)}, s32[]{:T(128)}, ...), condition=%wide.region_31.32_spmd.clone, body=%wide.region_30.31_spmd.clone.sunk | while | flops 75666432 | bytes 608343 | solution.py:101
  175.0 12.2 %all_gather.23 = f32[4,6,2048]{2,1,0:T(8,128)S(1)} all-gather(f32[1,6,2048]{2,1,0:T(8,128)S(1)} %all_gather_reshape.11), channel_id=1, replica_groups=mesh['row'=4,'col'=8] {'row'}, dimensions={0}, use_global_device_ids=true | all-gather | bytes 245760 | tf_op jit(solution)/shard_map/all_gather | solution.py:128
  187.2 0.6 multiply_reduce_fusion.9
  187.9 41.5 %all-reduce = (f32[]{:T(128)}, f32[]{:T(128)}) all-reduce(f32[]{:T(128)} %get-tuple-element.390, f32[]{:T(128)} %get-tuple-element.389), channel_id=1, replica_groups=mesh['row'=4,'col'=8] {'row','col'}, use_global_device_ids=true, to_apply=%region_25.26 | all-reduce | flops 2 | bytes 16 | tf_op jit(solution)/shard_map/psum | solution.py:106
  233.3 0.6 multiply_subtract_fusion
  (337 shorter events, 23.5 us)
Async XLA Ops:
  0.6 1.1 copy-start.1
  1.7 0.7 copy-start.2
  10.8 0.7 copy-start.3
  12.2 4.0 %copy-start = (f32[1,1,36,4096]{3,1,2,0:T(1,128)S(1)}, f32[1,1,36,4096]{3,1,2,0:T(1,128)}, u32[]{:S(2)}) copy-start(f32[1,1,36,4096]{3,1,2,0:T(1,128)} %param.20) | copy-start | bytes 1769476
  18.6 0.7 copy-start.4
